TPU v7x, 128 devices: a whole 4x4x4 slice. The times are simulated.
128 devices in a mesh: gx: 8 (over x, core), gy: 16 (over z, y).
Axes of the slice: x: 4, y: 4, z: 4, core: 2. Of those that a mesh axis runs over, the one named last changes fastest.
Arguments:
- record_keys: int32 [131072], P(('gx', 'gy')), may hold values from 0 to 16777215
- payloads: int32 [131072], P(('gx', 'gy')), may hold values from 0 to 16777215
Outputs:
- sorted_keys: int32 [245760], P(('gx', 'gy'))
- sorted_payloads: int32 [245760], P(('gx', 'gy'))
- bucket_sizes: int32 [128], P(('gx', 'gy'))
- bucket_digest: int32 [128], P(('gx', 'gy'))
All inputs are finite; a program needn't handle non-finite values.
Results may differ from a plain program's by a relative error of at most 0.000001.
Values may be sent and summed in bfloat16 or wider, within the bound.
A program may use at most 64 MiB of HBM per device.

v0:
```python
import jax
import jax.numpy as jnp
from jax import lax
from jax.sharding import PartitionSpec as P

filler = 1073741824


def in_order(blocks, dim):
    dims = list(blocks.shape[1:])
    dims[dim] *= blocks.shape[0]
    return jnp.moveaxis(blocks, 0, dim).reshape(dims)


def gather_packed(arrays, axis, dims):
    line = jnp.concatenate([a.reshape(-1) for a in arrays])
    lines, at, finished = lax.all_gather(line, axis), 0, []
    for a, dim in zip(arrays, dims):
        blocks = lines[:, at : at + a.size].reshape(-1, *a.shape)
        finished.append(in_order(blocks, dim))
        at += a.size
    return tuple(finished)


def beneath_grid(run_keys, run_places, split_keys, split_places):
    return (run_keys[None, :] < split_keys[:, None]) | (
        run_keys[None, :] == split_keys[:, None]
    ) & (run_places[None, :] <= split_places[:, None])


def shards(record_keys, payloads):
    devices = lax.axis_size(("gx", "gy"))
    per_device = record_keys.shape[0]
    spacing = per_device // devices
    bucket_cap = 2 * per_device - devices
    offset = lax.axis_index(("gx", "gy")) * per_device
    places = offset + lax.iota(jnp.int32, per_device)
    run_keys, run_places, run_values = lax.sort((record_keys, places, payloads), num_keys=2)
    sample_keys = run_keys.reshape(devices, spacing)[:, spacing - 1]
    sample_places = run_places.reshape(devices, spacing)[:, spacing - 1]
    every_keys, every_places = gather_packed((sample_keys, sample_places), ("gx", "gy"), (0, 0))
    every_keys, every_places = lax.sort((every_keys, every_places), num_keys=2)
    split_keys = every_keys.reshape(devices, devices)[: devices - 1, devices - 1]
    split_places = every_places.reshape(devices, devices)[: devices - 1, devices - 1]
    beneath = beneath_grid(run_keys, run_places, split_keys, split_places)
    bucket_of = devices - 1 - jnp.sum(beneath.astype(jnp.int32), axis=0)
    owners = lax.iota(jnp.int32, devices)
    mine = bucket_of[None, :] == owners[:, None]
    send_keys = jnp.where(mine, run_keys[None, :], filler)
    send_values = jnp.where(mine, run_values[None, :], filler)
    got_keys, got_values = (
        lax.all_to_all(send_keys, ("gx", "gy"), split_axis=0, concat_axis=0, tiled=True),
        lax.all_to_all(send_values, ("gx", "gy"), split_axis=0, concat_axis=0, tiled=True),
    )
    flat_keys, flat_values = lax.sort(
        (got_keys.reshape(-1), got_values.reshape(-1)), is_stable=True, num_keys=1
    )
    flat_keys = flat_keys[:bucket_cap]
    flat_values = flat_values[:bucket_cap]
    filled = flat_keys < filler
    sorted_keys = jnp.where(filled, flat_keys, -1)
    sorted_payloads = jnp.where(filled, flat_values, -1)
    bucket_size = jnp.sum(filled.astype(jnp.int32)).reshape(1)
    ranks = lax.iota(jnp.int32, bucket_cap)
    mixed = (sorted_keys + 3 * sorted_payloads + 5 * ranks) % 1024
    digest = jnp.sum(jnp.where(filled, 2 * mixed - 1023, 0)).astype(jnp.int32).reshape(1)
    return (sorted_keys, sorted_payloads, bucket_size, digest)


def solution(mesh):
    return jax.shard_map(
        shards,
        mesh=mesh,
        in_specs=(P(("gx", "gy")), P(("gx", "gy"))),
        out_specs=(P(("gx", "gy")), P(("gx", "gy")), P(("gx", "gy")), P(("gx", "gy"))),
        check_vma=False,
    )
```

profile of v0, /device:TPU:0, one launch (start us, length us, event | category | flops | bytes accessed | tf_op | source)
XLA Modules:
  0.0 215.1 jit_solution(15074508309098597869)
XLA Ops:
  7.2 0.0 sort.73.cloned.1.call-start
  7.2 0.0 copy-start
  7.2 0.0 copy-start.1
  7.3 0.6 copy-done
  7.9 0.0 copy-done.1
  7.9 4.5 %sort.69 = (s32[1024]{0:T(1024)S(1)}, s32[1024]{0:T(1024)S(1)}, s32[1024]{0:T(1024)S(1)}, s32[1024]{0:T(1024)}) sort(s32[1024]{0:T(1024)S(1)} %copy-done, s32[1024]{0:T(1024)S(1)} %iota_add_fusion, s32[1024]{0:T(1024)S(1)} %copy-done.1, s32[1024]{0:T(1024)S(1)} %iota.22), dimensions={0}, to_apply=%region_0.0 | sort | flops 10240 | bytes 32768 | tf_op jit(solution)/shard_map/sort | solution.py:38
  12.4 0.1 reshape.138
  12.5 0.1 reshape.137
  12.6 0.2 slice_reduce_fusion.2
  12.8 67.2 %all-gather.1 = s32[128,1,256]{2,1,0:T(1,128)S(1)} all-gather(s32[1,1,256]{2,1,0:T(1,128)S(1)} %bitcast.19), channel_id=2, replica_groups=mesh['gx'=8,'gy'=16] {'gx','gy'}, dimensions={0}, use_global_device_ids=true | all-gather | bytes 132096 | tf_op jit(solution)/shard_map/all_gather | solution.py:17
  80.1 8.5 %sort.70 = (s32[16384]{0:T(1024)S(1)}, s32[16384]{0:T(1024)S(1)}, s32[16384]{0:T(1024)}) sort(s32[16384]{0:T(1024)S(1)} %get-tuple-element.28, s32[16384]{0:T(1024)S(1)} %get-tuple-element.27, s32[16384]{0:T(1024)S(1)} %iota.23), dimensions={0}, to_apply=%region_1.0 | sort | flops 229376 | bytes 393216 | tf_op jit(solution)/shard_map/sort | solution.py:42
  88.5 0.2 slice_reduce_fusion.1
  88.7 0.2 slice_reduce_fusion
  88.9 0.2 convert_reduce_fusion
  89.1 0.7 compare_select_fusion
  89.8 20.2 %all_to_all.12 = s32[128,1,1024]{2,1,0:T(1,128)} all-to-all(s32[128,1,1024]{2,1,0:T(1,128)S(1)} %get-tuple-element.29), channel_id=1, replica_groups=mesh['gx'=8,'gy'=16] {'gx','gy'}, dimensions={0} | all-to-all | bytes 1048576 | tf_op jit(solution)/shard_map/all_to_all | solution.py:53
  110.0 18.2 %all_to_all.13 = s32[128,1,1024]{2,1,0:T(1,128)} all-to-all(s32[128,1,1024]{2,1,0:T(1,128)S(1)} %get-tuple-element.30), channel_id=1, replica_groups=mesh['gx'=8,'gy'=16] {'gx','gy'}, dimensions={0} | all-to-all | bytes 1048576 | tf_op jit(solution)/shard_map/all_to_all | solution.py:52
  128.2 0.0 sort.73.cloned.1.call-update
  128.2 78.0 %sort.73.cloned.1.call-done = (s32[131072]{0:T(1024)}, s32[131072]{0:T(1024)}) async-done(((s32[131072]{0:T(1024)}, s32[131072]{0:T(1024)}), (s32[131072]{0:T(1024)}, s32[131072]{0:T(1024)})) %sort.73.cloned.1.call-update) | async-done | bytes 1048592 | tf_op jit(solution)/shard_map/sort | solution.py:55
  206.3 2.0 fusion.4
  (7 shorter events, 0.0 us)
Async XLA Ops:
  7.2 199.1 %sort.73.cloned.1.call-start = ((), (), s32[]{:S(2)}) async-start(), calls=%async_computation.2 | async-start | bytes 3145760 | tf_op jit(solution)/shard_map/sort | solution.py:55
  7.2 0.7 copy-start
  7.2 0.7 copy-start.1
Sparse Core Ops, SparseCore 0:
  128.4 77.8 sort.75.cloned.1.call-done
  (1 shorter events, 0.0 us)
where the time goes:
time: 218 us; the launch traced here: 215 us
  blocking collectives  106 us (49%)
  local copies, waits for them, and re-layouts  79.4 us (36%)
  other arithmetic  15.8 us (7%)
  between operations  14.1 us (6%)
    sort x2, local copies, waits for them, and re-layouts, shards(): lax.sort((got_keys.reshape(-1), got_values.reshape(-1)), is_stable=True,...  78 us
    all_gather x1, blocking collectives, gather_packed(): lines, at, finished = (lax.all_gather(line, axis), 0, [])  67.2 us
    all_to_all x1, blocking collectives, shards(): lax.all_to_all(send_values, ('gx', 'gy'), split_axis=0, concat_axis=0, ti...  20.2 us
    all_to_all x1, blocking collectives, shards(): lax.all_to_all(send_keys, ('gx', 'gy'), split_axis=0, concat_axis=0, tile...  18.2 us
    sort x1, other arithmetic, shards(): every_keys, every_places = lax.sort((every_keys, every_places), num_keys=2)  8.46 us
    sort x1, other arithmetic, shards(): lax.sort((record_keys, places, payloads), num_keys=2)  4.52 us

commit v1 on v0

v1 whole, which is shorter than its diff:
```python
import functools

import jax
import jax.numpy as jnp
from jax import lax
from jax.experimental import pallas as pl
from jax.experimental.pallas import tpu as pltpu
from jax.sharding import PartitionSpec as P

MESH = pl.DeviceIdType.MESH
LANES = 128
SUBS = 8
CHUNK = 256
CHUNKS = 3
BIG = 1 << 24
f32, bf16, i32 = jnp.float32, jnp.bfloat16, jnp.int32


def iota(shape, dim):
    return lax.broadcasted_iota(i32, shape, dim)


def row(x, s):
    return jnp.broadcast_to(x[s : s + 1, :], (SUBS, LANES))


def pieces(x):
    return [x & (CHUNK - 1), (x >> 8) & (CHUNK - 1), x >> 16]


def joined(parts):
    parts = [p.astype(i32) for p in parts]
    return parts[0] + (parts[1] << 8) + (parts[2] << 16)


def placed(rows, his, los, count):
    left, right = [], []
    for (keys, values), hi, lo in zip(rows, his, los):
        parts = [p.astype(f32) for p in pieces(keys) + pieces(values)]
        for s in range(SUBS):
            onehot = jnp.broadcast_to(lo[s : s + 1, :], (LANES, LANES)) == iota((LANES, LANES), 0)
            right.append(jnp.where(onehot, 1.0, 0.0).astype(bf16))
            column = []
            at = jnp.broadcast_to(hi[s : s + 1, :], (count, LANES)) == iota((count, LANES), 0)
            for p in parts:
                column.append(jnp.where(at, jnp.broadcast_to(p[s : s + 1, :], (count, LANES)), 0.0))
            left.append(jnp.concatenate(column, axis=0).astype(bf16))
    left = jnp.concatenate(left, axis=1)
    right = jnp.concatenate(right, axis=1)
    out = lax.dot_general(left, right, (((1,), (1,)), ((), ())), preferred_element_type=f32)
    out = [out[c * count : (c + 1) * count, :] for c in range(2 * CHUNKS)]
    return joined(out[:CHUNKS]), joined(out[CHUNKS:])


def sublane_sums(accs):
    return jnp.concatenate([jnp.sum(a, axis=0, keepdims=True) for a in accs], axis=0)


STEP = 16


def block_ranks(keys):
    subs, lanes = iota((SUBS, LANES), 0), iota((SUBS, LANES), 1)
    rows = [row(keys, s) + jnp.where(subs < s, 1, 0) for s in range(SUBS)]

    def body(t, carry):
        turned, accs, ties = carry
        accs = list(accs)
        for m in range(STEP):
            one = jnp.broadcast_to(turned[:, m : m + 1], (SUBS, LANES))
            for s in range(SUBS):
                accs[s] = accs[s] + jnp.where(one < rows[s], 1, 0)
            ties = ties + jnp.where((one == keys) & (lanes > t * STEP + m), 1, 0)
        return pltpu.roll(turned, LANES - STEP, 1), tuple(accs), ties

    zero = jnp.zeros((SUBS, LANES), i32)
    _, accs, ties = lax.fori_loop(0, LANES // STEP, body, (keys, (zero,) * SUBS, zero))
    return sublane_sums(accs) + ties


def candidate_ranks(halves):
    subs, lanes = iota((SUBS, LANES), 0), iota((SUBS, LANES), 1)
    rows = [[row(k, s) for s in range(SUBS)] for k in halves]
    zero = jnp.zeros((SUBS, LANES), i32)
    accs = [[zero] * SUBS for _ in halves]
    for source, keys in enumerate(halves):

        def body(t, carry, source=source):
            turned, accs = carry
            accs = [list(a) for a in accs]
            for m in range(STEP):
                one = jnp.broadcast_to(turned[:, m : m + 1], (SUBS, LANES))
                for target in range(2):
                    less = one
                    if target == source:
                        less = one - jnp.where(lanes > t * STEP + m, 1, 0)
                    elif target > source:
                        less = one - 1
                    for s in range(SUBS):
                        accs[target][s] = accs[target][s] + jnp.where(less < rows[target][s], 1, 0)
            return pltpu.roll(turned, LANES - STEP, 1), tuple(tuple(a) for a in accs)

        _, accs = lax.fori_loop(0, LANES // STEP, body, (keys, tuple(tuple(a) for a in accs)))
    ranks = []
    for keys, acc in zip(halves, accs):
        ties = zero
        for d in range(1, SUBS):
            ties = ties + jnp.where((pltpu.roll(keys, d, 0) == keys) & (subs >= d), 1, 0)
        ranks.append(sublane_sums(acc) + ties)
    return ranks


def sorted_block(keys, values):
    rank = block_ranks(keys)
    return placed([(keys, values)], [rank & (SUBS - 1)], [rank >> 3], SUBS)


def gather_kernel(xs, planes, keys_ref, values_ref, out_ref, block, local_sem, send_sem, recv_sem, give_sem, take_sem):
    gx, gy = lax.axis_index("gx"), lax.axis_index("gy")
    x, core = gx // 2, gx % 2
    partner = x * 2 + (1 - core)
    barrier = pltpu.get_barrier_semaphore()

    def others():
        for dx in range(xs):
            for dy in range(planes):
                if dx or dy:
                    yield dx, dy

    def device(dx, dy):
        return ((x + dx) % xs) * 2 + core, (gy + dy) % planes

    for dx, dy in others():
        pl.semaphore_signal(barrier, inc=1, device_id=device(dx, dy), device_id_type=MESH)
    pl.semaphore_signal(barrier, inc=1, device_id=(partner, gy), device_id_type=MESH)

    keys, values = sorted_block(keys_ref[...], values_ref[...])
    block[0:SUBS, :] = keys
    block[SUBS : 2 * SUBS, :] = values
    pl.semaphore_wait(barrier, xs * planes)

    me = gx * planes + gy
    mine = pltpu.make_async_copy(block, out_ref.at[me], local_sem)
    mine.start()
    sends = []
    for dx, dy in others():
        copy = pltpu.make_async_remote_copy(
            src_ref=block,
            dst_ref=out_ref.at[me],
            send_sem=send_sem,
            recv_sem=recv_sem.at[(xs - dx) % xs],
            device_id=device(dx, dy),
            device_id_type=MESH,
        )
        copy.start()
        sends.append(copy)
    mine.wait()
    gives = []
    for dx in range(xs):
        at = pl.multiple_of((((x + dx) % xs) * 2 + core) * planes, planes)
        count = planes if dx else planes - 1
        arrived = out_ref.at[pl.ds(at, count)]
        pltpu.make_async_copy(arrived, arrived, recv_sem.at[dx]).wait()
        group = out_ref.at[pl.ds(at, planes)]
        give = pltpu.make_async_remote_copy(
            src_ref=group,
            dst_ref=group,
            send_sem=give_sem.at[dx],
            recv_sem=take_sem.at[dx],
            device_id=(partner, gy),
            device_id_type=MESH,
        )
        give.start()
        gives.append(give)
    sent = out_ref.at[pl.ds(0, xs * planes - 1)]
    pltpu.make_async_copy(sent, sent, send_sem).wait()
    for give in gives:
        give.wait()


def splitter_key(samples_ref, wanted):
    subs = iota((SUBS, LANES), 0)
    base = [jnp.zeros((SUBS, LANES), i32) for _ in wanted]
    for shift in range(21, -1, -3):
        tests = [b + ((subs + 1) << shift) for b in base]
        zero = jnp.zeros((SUBS, LANES), i32)

        def body(t, accs):
            accs = list(accs)
            for r in range(SUBS):
                one = jnp.broadcast_to(samples_ref[pl.ds(t * SUBS + r, 1), :], (SUBS, LANES))
                for n in range(len(tests)):
                    accs[n] = accs[n] + jnp.where(one < tests[n], 1, 0)
            return tuple(accs)

        accs = lax.fori_loop(0, LANES // SUBS, body, (zero,) * len(wanted))
        for n in range(len(wanted)):
            below = jnp.sum(accs[n].astype(f32), axis=1, keepdims=True)
            passed = jnp.where((below < wanted[n].astype(f32)) & (subs[:, :1] < SUBS - 1), 1, 0)
            digit = jnp.sum(passed, axis=0, keepdims=True)
            base[n] = base[n] + (jnp.broadcast_to(digit, (SUBS, LANES)) << shift)
    return base


def bucket_kernel(blocks_ref, keys_out, values_out, info_out, samples_ref, turn_ref, in_ref):
    devices = blocks_ref.shape[0]
    d = lax.axis_index("gx") * lax.axis_size("gy") + lax.axis_index("gy")
    square = (LANES, LANES)
    samples_ref[...] = blocks_ref[:, SUBS - 1, :]
    wanted = [d * LANES, (d + 1) * LANES]
    low, high = splitter_key(samples_ref, wanted)
    high = jnp.where(d == devices - 1, BIG, high)
    samples = samples_ref[...]
    ends = [jnp.broadcast_to(k[:1, :], square) for k in (low, high)]
    ones = jnp.ones(square, bf16)
    below = jnp.where(iota(square, 1) < iota(square, 0), 1.0, 0.0).astype(bf16)

    def mm(a, b):
        return jnp.dot(a, b, preferred_element_type=f32)

    masks = []
    for k in ends:
        masks += [samples < k, samples <= k]
    counts = mm(jnp.concatenate([jnp.where(m, 1.0, 0.0).astype(bf16) for m in masks], axis=0), ones)
    counts = [counts[n * LANES : (n + 1) * LANES, :] for n in range(4)]
    taken, tied = [], []
    for n in range(2):
        lt, le = counts[2 * n], counts[2 * n + 1]
        equal = le - lt
        before = mm(below, equal.astype(bf16))
        total = mm(ones, lt.astype(bf16))
        left = jnp.asarray(wanted[n], f32) - total - before
        taken.append(lt + jnp.clip(left, 0.0, equal))
        tied.append(jnp.where(left > equal, 1, 0))
    first = taken[0]
    number = jnp.minimum(taken[1], LANES - 1.0) - first + 1.0
    start = mm(below, number.astype(bf16)).astype(i32)
    number, first, last = number.astype(i32), first.astype(i32), taken[1].astype(i32)
    lanes = iota(square, 1)
    turn_ref[...] = (lanes - (start - first)) & (LANES - 1)
    codes = []
    for h in range(2):
        m = lanes + h * LANES
        inside = (m >= start) & (m < start + number)
        in_ref[h] = jnp.where(inside, 1, 0)
        code = jnp.where(inside, 16, 0)
        code = code + jnp.where(inside & (m == start), 1 + tied[0], 0)
        code = code + jnp.where(inside & (m == start + last - first), 4 * (1 + tied[1]), 0)
        codes.append(code.astype(f32).astype(bf16))
    codes = mm(jnp.ones((SUBS, LANES), bf16), jnp.concatenate(codes, axis=1)).astype(i32)

    zero = jnp.zeros((SUBS, LANES), i32)

    def body(t, carry):
        carry = list(carry)
        for r in range(SUBS):
            b = t * SUBS + r
            turn = jnp.broadcast_to(turn_ref[pl.ds(b, 1), :], (SUBS, LANES))
            for c in range(2):
                tile = blocks_ref[b, c * SUBS : (c + 1) * SUBS, :]
                tile = jnp.take_along_axis(tile, turn, axis=1, mode="promise_in_bounds")
                for h in range(2):
                    inside = jnp.broadcast_to(in_ref[h, pl.ds(b, 1), :], (SUBS, LANES)) > 0
                    carry[2 * c + h] = jnp.where(inside, tile, carry[2 * c + h])
        return tuple(carry)

    k0, k1, v0, v1 = lax.fori_loop(0, devices // SUBS, body, (zero,) * 4)
    keys, valid = [], []
    for h, k in enumerate((k0, k1)):
        code = codes[:, h * LANES : (h + 1) * LANES]
        is_low, is_high = code & 3, (code >> 2) & 3
        ok = code >= 16
        ok = ok & ((is_low == 0) | (k >= low + is_low - 1))
        ok = ok & ((is_high == 0) | (k < high + is_high - 1))
        valid.append(jnp.where(ok, 1, 0))
        keys.append(jnp.where(ok, k, BIG))
    size = jnp.sum(jnp.sum(valid[0] + valid[1], axis=1, keepdims=True), axis=0, keepdims=True)
    ranks = candidate_ranks(keys)
    count = 2 * SUBS
    keys, values = placed(
        [(keys[0], v0), (keys[1], v1)], [r >> 7 for r in ranks], [r & (LANES - 1) for r in ranks], count
    )
    rank = iota((count, LANES), 0) * LANES + iota((count, LANES), 1)
    filled = rank < size
    keys = jnp.where(filled, keys, -1)
    values = jnp.where(filled, values, -1)
    keys_out[...] = keys[: keys_out.shape[0], :]
    values_out[...] = values[: values_out.shape[0], :]
    mixed = (keys + 3 * values + 5 * rank) & 1023
    digest = jnp.where(filled, 2 * mixed - 1023, 0)
    digest = jnp.sum(jnp.sum(digest, axis=1, keepdims=True), axis=0, keepdims=True)
    sub = iota((SUBS, LANES), 0)
    info_out[...] = jnp.where(sub == 0, size, digest)


def gathered(keys, values, xs, planes):
    blocks = 2 * xs * planes
    return pl.pallas_call(
        functools.partial(gather_kernel, xs, planes),
        out_shape=jax.ShapeDtypeStruct((blocks, 2 * SUBS, LANES), i32),
        in_specs=[pl.BlockSpec(memory_space=pltpu.VMEM)] * 2,
        out_specs=pl.BlockSpec(memory_space=pl.ANY),
        scratch_shapes=[
            pltpu.VMEM((2 * SUBS, LANES), i32),
            pltpu.SemaphoreType.DMA,
            pltpu.SemaphoreType.DMA,
            pltpu.SemaphoreType.DMA((xs,)),
            pltpu.SemaphoreType.DMA((xs,)),
            pltpu.SemaphoreType.DMA((xs,)),
        ],
        compiler_params=pltpu.CompilerParams(collective_id=0, has_side_effects=True),
        name="gather_blocks",
    )(keys, values)


def bucket(blocks, rows):
    devices = blocks.shape[0]
    return pl.pallas_call(
        bucket_kernel,
        out_shape=(
            jax.ShapeDtypeStruct((rows, LANES), i32),
            jax.ShapeDtypeStruct((rows, LANES), i32),
            jax.ShapeDtypeStruct((SUBS, LANES), i32),
        ),
        in_specs=[pl.BlockSpec(memory_space=pltpu.VMEM)],
        out_specs=[pl.BlockSpec(memory_space=pltpu.VMEM)] * 3,
        scratch_shapes=[
            pltpu.VMEM((devices, LANES), i32),
            pltpu.VMEM((devices, LANES), i32),
            pltpu.VMEM((2, devices, LANES), i32),
        ],
        name="make_bucket",
    )(blocks)


def solution(mesh):
    gx, gy = mesh.shape["gx"], mesh.shape["gy"]

    def shards(record_keys, payloads):
        keys = record_keys.reshape(SUBS, LANES)
        values = payloads.reshape(SUBS, LANES)
        blocks = gathered(keys, values, gx // 2, gy)
        rows = (2 * record_keys.shape[0] - gx * gy) // LANES
        sorted_keys, sorted_values, info = bucket(blocks, rows)
        return (sorted_keys.reshape(-1), sorted_values.reshape(-1), info[0, :1], info[1, :1])

    spec = P(("gx", "gy"))
    return jax.shard_map(shards, mesh=mesh, in_specs=(spec,) * 2, out_specs=(spec,) * 4, check_vma=False)
```

time: 218 us -> 33.4 us (0.15)
  the two profiles are of different devices: /device:TPU:0 before, /device:TPU:1 now
where the time goes in v1:
time: 33.4 us; the launch traced here: 33.1 us
  Pallas kernels  31.2 us (93%)
  local copies, waits for them, and re-layouts  1.26 us (4%)
  between operations  0.64 us (2%)
    pallas_call x1, Pallas kernels, gathered(): pl.pallas_call(functools.partial(gather_kernel, xs, planes), out_shape=ja...  21.4 us
    pallas_call x1, Pallas kernels, bucket(): pl.pallas_call(bucket_kernel, out_shape=(jax.ShapeDtypeStruct((rows, LANE...  9.83 us
    slice x1, local copies, waits for them, and re-layouts, shards(): info[1, :1]  1.26 us

profile of v1, /device:TPU:1, one launch (start us, length us, event | category | flops | bytes accessed | tf_op | source)
XLA Modules:
  0.0 33.1 jit_solution(6579400929480796487)
XLA Ops:
  0.6 21.4 %gather_blocks.1.blocks_ref = s32[128,16,128]{2,1,0:T(8,128)} custom-call(s32[8,128]{1,0:T(8,128)} %bitcast.6, s32[8,128]{1,0:T(8,128)} %bitcast.7), custom_call_target="tpu_custom_call" | custom-call | tf_op jit(solution)/shard_map/gather_blocks/pallas_call | solution.py:298
  22.0 9.8 %make_bucket.1 = (s32[15,128]{1,0:T(8,128)}, s32[15,128]{1,0:T(8,128)}, s32[8,128]{1,0:T(8,128)}) custom-call(s32[128,16,128]{2,1,0:T(8,128)} %gather_blocks.1.blocks_ref), custom_call_target="tpu_custom_call" | custom-call | tf_op jit(solution)/shard_map/make_bucket/pallas_call | solution.py:318
  31.9 1.3 %fusion = (s32[1,1]{1,0:T(1,128)}, s32[1,1]{1,0:T(1,128)}) fusion(s32[8,128]{1,0:T(8,128)} %get-tuple-element.9), kind=kLoop, calls=%fused_computation | loop fusion | bytes 16 | tf_op jit(solution)/shard_map/slice | solution.py:345

commit v2 on v1

--- a/solution.py
+++ b/solution.py
@@ -115,7 +115,9 @@
     return placed([(keys, values)], [rank & (SUBS - 1)], [rank >> 3], SUBS)
 
 
-def gather_kernel(xs, planes, keys_ref, values_ref, out_ref, block, local_sem, send_sem, recv_sem, give_sem, take_sem):
+def gather_kernel(
+    xs, planes, keys_ref, values_ref, found_ref, block, blocks, samples, turns, inside, send_sem, recv_sem, give_sem, take_sem
+):
     gx, gy = lax.axis_index("gx"), lax.axis_index("gy")
     x, core = gx // 2, gx % 2
     partner = x * 2 + (1 - core)
@@ -134,34 +136,29 @@
         pl.semaphore_signal(barrier, inc=1, device_id=device(dx, dy), device_id_type=MESH)
     pl.semaphore_signal(barrier, inc=1, device_id=(partner, gy), device_id_type=MESH)
 
+    me = gx * planes + gy
     keys, values = sorted_block(keys_ref[...], values_ref[...])
-    block[0:SUBS, :] = keys
-    block[SUBS : 2 * SUBS, :] = values
+    for ref in (block, blocks.at[me]):
+        ref[0:SUBS, :] = keys
+        ref[SUBS : 2 * SUBS, :] = values
     pl.semaphore_wait(barrier, xs * planes)
 
-    me = gx * planes + gy
-    mine = pltpu.make_async_copy(block, out_ref.at[me], local_sem)
-    mine.start()
-    sends = []
     for dx, dy in others():
-        copy = pltpu.make_async_remote_copy(
+        pltpu.make_async_remote_copy(
             src_ref=block,
-            dst_ref=out_ref.at[me],
+            dst_ref=blocks.at[me],
             send_sem=send_sem,
             recv_sem=recv_sem.at[(xs - dx) % xs],
             device_id=device(dx, dy),
             device_id_type=MESH,
-        )
-        copy.start()
-        sends.append(copy)
-    mine.wait()
+        ).start()
     gives = []
     for dx in range(xs):
         at = pl.multiple_of((((x + dx) % xs) * 2 + core) * planes, planes)
         count = planes if dx else planes - 1
-        arrived = out_ref.at[pl.ds(at, count)]
+        arrived = blocks.at[pl.ds(at, count)]
         pltpu.make_async_copy(arrived, arrived, recv_sem.at[dx]).wait()
-        group = out_ref.at[pl.ds(at, planes)]
+        group = blocks.at[pl.ds(at, planes)]
         give = pltpu.make_async_remote_copy(
             src_ref=group,
             dst_ref=group,
@@ -172,10 +169,15 @@
         )
         give.start()
         gives.append(give)
-    sent = out_ref.at[pl.ds(0, xs * planes - 1)]
+    for give in gives:
+        give.wait_recv()
+    keys, values = select(blocks, samples, turns, inside)
+    for n, tile in enumerate(keys + values):
+        found_ref[n * SUBS : (n + 1) * SUBS, :] = tile
+    sent = blocks.at[pl.ds(0, xs * planes - 1)]
     pltpu.make_async_copy(sent, sent, send_sem).wait()
     for give in gives:
-        give.wait()
+        give.wait_send()
 
 
 def splitter_key(samples_ref, wanted):
@@ -202,7 +204,7 @@
     return base
 
 
-def bucket_kernel(blocks_ref, keys_out, values_out, info_out, samples_ref, turn_ref, in_ref):
+def select(blocks_ref, samples_ref, turn_ref, in_ref):
     devices = blocks_ref.shape[0]
     d = lax.axis_index("gx") * lax.axis_size("gy") + lax.axis_index("gy")
     square = (LANES, LANES)
@@ -274,11 +276,18 @@
         ok = ok & ((is_high == 0) | (k < high + is_high - 1))
         valid.append(jnp.where(ok, 1, 0))
         keys.append(jnp.where(ok, k, BIG))
-    size = jnp.sum(jnp.sum(valid[0] + valid[1], axis=1, keepdims=True), axis=0, keepdims=True)
+    return keys, [v0, v1]
+
+
+def place_kernel(found_ref, keys_out, values_out, size_out, digest_out):
+    found = [found_ref[n * SUBS : (n + 1) * SUBS, :] for n in range(4)]
+    keys, values = found[:2], found[2:]
+    valid = jnp.where(keys[0] < BIG, 1, 0) + jnp.where(keys[1] < BIG, 1, 0)
+    size = jnp.sum(jnp.sum(valid, axis=1, keepdims=True), axis=0, keepdims=True)
     ranks = candidate_ranks(keys)
     count = 2 * SUBS
     keys, values = placed(
-        [(keys[0], v0), (keys[1], v1)], [r >> 7 for r in ranks], [r & (LANES - 1) for r in ranks], count
+        list(zip(keys, values)), [r >> 7 for r in ranks], [r & (LANES - 1) for r in ranks], count
     )
     rank = iota((count, LANES), 0) * LANES + iota((count, LANES), 1)
     filled = rank < size
@@ -289,48 +298,43 @@
     mixed = (keys + 3 * values + 5 * rank) & 1023
     digest = jnp.where(filled, 2 * mixed - 1023, 0)
     digest = jnp.sum(jnp.sum(digest, axis=1, keepdims=True), axis=0, keepdims=True)
-    sub = iota((SUBS, LANES), 0)
-    info_out[...] = jnp.where(sub == 0, size, digest)
-
-
-def gathered(keys, values, xs, planes):
+    size_out[0] = size[0, 0]
+    digest_out[0] = digest[0, 0]
+
+
+def candidates(keys, values, xs, planes):
     blocks = 2 * xs * planes
+    dma = pltpu.SemaphoreType.DMA
     return pl.pallas_call(
         functools.partial(gather_kernel, xs, planes),
-        out_shape=jax.ShapeDtypeStruct((blocks, 2 * SUBS, LANES), i32),
+        out_shape=jax.ShapeDtypeStruct((4 * SUBS, LANES), i32),
         in_specs=[pl.BlockSpec(memory_space=pltpu.VMEM)] * 2,
-        out_specs=pl.BlockSpec(memory_space=pl.ANY),
+        out_specs=pl.BlockSpec(memory_space=pltpu.VMEM),
         scratch_shapes=[
             pltpu.VMEM((2 * SUBS, LANES), i32),
-            pltpu.SemaphoreType.DMA,
-            pltpu.SemaphoreType.DMA,
-            pltpu.SemaphoreType.DMA((xs,)),
-            pltpu.SemaphoreType.DMA((xs,)),
-            pltpu.SemaphoreType.DMA((xs,)),
+            pltpu.VMEM((blocks, 2 * SUBS, LANES), i32),
+            pltpu.VMEM((blocks, LANES), i32),
+            pltpu.VMEM((blocks, LANES), i32),
+            pltpu.VMEM((2, blocks, LANES), i32),
+            dma,
+            dma((xs,)),
+            dma((xs,)),
+            dma((xs,)),
         ],
         compiler_params=pltpu.CompilerParams(collective_id=0, has_side_effects=True),
-        name="gather_blocks",
+        name="find_candidates",
     )(keys, values)
 
 
-def bucket(blocks, rows):
-    devices = blocks.shape[0]
+def placed_bucket(found, rows):
+    one = jax.ShapeDtypeStruct((1,), i32)
     return pl.pallas_call(
-        bucket_kernel,
-        out_shape=(
-            jax.ShapeDtypeStruct((rows, LANES), i32),
-            jax.ShapeDtypeStruct((rows, LANES), i32),
-            jax.ShapeDtypeStruct((SUBS, LANES), i32),
-        ),
+        place_kernel,
+        out_shape=(jax.ShapeDtypeStruct((rows, LANES), i32),) * 2 + (one, one),
         in_specs=[pl.BlockSpec(memory_space=pltpu.VMEM)],
-        out_specs=[pl.BlockSpec(memory_space=pltpu.VMEM)] * 3,
-        scratch_shapes=[
-            pltpu.VMEM((devices, LANES), i32),
-            pltpu.VMEM((devices, LANES), i32),
-            pltpu.VMEM((2, devices, LANES), i32),
-        ],
-        name="make_bucket",
-    )(blocks)
+        out_specs=[pl.BlockSpec(memory_space=pltpu.VMEM)] * 2 + [pl.BlockSpec(memory_space=pltpu.SMEM)] * 2,
+        name="place_bucket",
+    )(found)
 
 
 def solution(mesh):
@@ -339,10 +343,10 @@
     def shards(record_keys, payloads):
         keys = record_keys.reshape(SUBS, LANES)
         values = payloads.reshape(SUBS, LANES)
-        blocks = gathered(keys, values, gx // 2, gy)
+        found = candidates(keys, values, gx // 2, gy)
         rows = (2 * record_keys.shape[0] - gx * gy) // LANES
-        sorted_keys, sorted_values, info = bucket(blocks, rows)
-        return (sorted_keys.reshape(-1), sorted_values.reshape(-1), info[0, :1], info[1, :1])
+        sorted_keys, sorted_values, size, digest = placed_bucket(found, rows)
+        return sorted_keys.reshape(-1), sorted_values.reshape(-1), size, digest
 
     spec = P(("gx", "gy"))
     return jax.shard_map(shards, mesh=mesh, in_specs=(spec,) * 2, out_specs=(spec,) * 4, check_vma=False)

time: 33.4 us -> 31.7 us (0.949)
  local copies, waits for them, and re-layouts: 1.26 us -> 0 us
  Pallas kernels: 31.2 us -> 30.8 us
    slice x1 -> x0, local copies, waits for them, and re-layouts: 1.26 us -> none  [shards(): info[1, :1]]
    pallas_call x2, Pallas kernels: 31.2 us -> 30.8 us  [the longest x1 26.1 us: candidates(): pl.pallas_call(functools.partial(gather_kernel, xs, planes), out_shape=ja...]
where the time goes in v2:
time: 31.7 us; the launch traced here: 31.4 us
  Pallas kernels  30.8 us (97%)
  between operations  0.64 us (2%)
    pallas_call x1, Pallas kernels, candidates(): pl.pallas_call(functools.partial(gather_kernel, xs, planes), out_shape=ja...  26.1 us
    pallas_call x1, Pallas kernels, placed_bucket(): pl.pallas_call(place_kernel, out_shape=(jax.ShapeDtypeStruct((rows, LANES...  4.71 us

profile of v2, /device:TPU:1, one launch (start us, length us, event | category | flops | bytes accessed | tf_op | source)
XLA Modules:
  0.0 31.4 jit_solution(6431241829976107932)
XLA Ops:
  0.6 26.1 %find_candidates.1.found_ref = s32[32,128]{1,0:T(8,128)} custom-call(s32[8,128]{1,0:T(8,128)} %bitcast.4, s32[8,128]{1,0:T(8,128)} %bitcast.5), custom_call_target="tpu_custom_call" | custom-call | tf_op jit(solution)/shard_map/find_candidates/pallas_call | solution.py:308
  26.7 4.7 %place_bucket.1 = (s32[15,128]{1,0:T(8,128)}, s32[15,128]{1,0:T(8,128)}, s32[1]{0:T(128)}, s32[1]{0:T(128)}) custom-call(s32[32,128]{1,0:T(8,128)} %find_candidates.1.found_ref), custom_call_target="tpu_custom_call" | custom-call | tf_op jit(solution)/shard_map/place_bucket/pallas_call | solution.py:331

commit v3 on v2

v3 whole, which is shorter than its diff:
```python
import functools

import jax
import jax.numpy as jnp
from jax import lax
from jax.experimental import pallas as pl
from jax.experimental.pallas import tpu as pltpu
from jax.sharding import PartitionSpec as P

MESH = pl.DeviceIdType.MESH
LANES = 128
SUBS = 8
CHUNK = 256
CHUNKS = 3
BIG = 1 << 24
f32, bf16, i32 = jnp.float32, jnp.bfloat16, jnp.int32


def iota(shape, dim):
    return lax.broadcasted_iota(i32, shape, dim)


def row(x, s):
    return jnp.broadcast_to(x[s : s + 1, :], (SUBS, LANES))


def pieces(x):
    return [x & (CHUNK - 1), (x >> 8) & (CHUNK - 1), x >> 16]


def joined(parts):
    parts = [p.astype(i32) for p in parts]
    return parts[0] + (parts[1] << 8) + (parts[2] << 16)


def placed(rows, his, los, count):
    left, right = [], []
    for (keys, values), hi, lo in zip(rows, his, los):
        parts = [p.astype(f32) for p in pieces(keys) + pieces(values)]
        for s in range(SUBS):
            onehot = jnp.broadcast_to(lo[s : s + 1, :], (LANES, LANES)) == iota((LANES, LANES), 0)
            right.append(jnp.where(onehot, 1.0, 0.0).astype(bf16))
            column = []
            at = jnp.broadcast_to(hi[s : s + 1, :], (count, LANES)) == iota((count, LANES), 0)
            for p in parts:
                column.append(jnp.where(at, jnp.broadcast_to(p[s : s + 1, :], (count, LANES)), 0.0))
            left.append(jnp.concatenate(column, axis=0).astype(bf16))
    left = jnp.concatenate(left, axis=1)
    right = jnp.concatenate(right, axis=1)
    out = lax.dot_general(left, right, (((1,), (1,)), ((), ())), preferred_element_type=f32)
    out = [out[c * count : (c + 1) * count, :] for c in range(2 * CHUNKS)]
    return joined(out[:CHUNKS]), joined(out[CHUNKS:])


def sublane_sums(accs):
    return jnp.concatenate([jnp.sum(a, axis=0, keepdims=True) for a in accs], axis=0)


def column(x, m):
    return jnp.broadcast_to(x[:, m : m + 1], (SUBS, LANES))


def block_ranks(keys):
    subs, lanes = iota((SUBS, LANES), 0), iota((SUBS, LANES), 1)
    rows = [row(keys, s) + jnp.where(subs < s, 1, 0) for s in range(SUBS)]
    zero = jnp.zeros((SUBS, LANES), i32)
    accs, ties = [zero] * SUBS, zero
    for m in range(LANES):
        one = column(keys, m)
        for s in range(SUBS):
            accs[s] = accs[s] + jnp.where(one < rows[s], 1, 0)
        ties = ties + jnp.where((one == keys) & (lanes > m), 1, 0)
    return sublane_sums(accs) + ties


def candidate_ranks(halves):
    subs, lanes = iota((SUBS, LANES), 0), iota((SUBS, LANES), 1)
    zero = jnp.zeros((SUBS, LANES), i32)
    ranks = []
    for target, keys in enumerate(halves):
        rows = [row(keys, s) for s in range(SUBS)]
        accs = [zero] * SUBS
        for source, others in enumerate(halves):
            if target > source:
                others = others - 1
            for m in range(LANES):
                one = column(others, m)
                if target == source:
                    one = one - jnp.where(lanes > m, 1, 0)
                for s in range(SUBS):
                    accs[s] = accs[s] + jnp.where(one < rows[s], 1, 0)
        ties = zero
        for d in range(1, SUBS):
            ties = ties + jnp.where((pltpu.roll(keys, d, 0) == keys) & (subs >= d), 1, 0)
        ranks.append(sublane_sums(accs) + ties)
    return ranks


def sorted_block(keys, values):
    rank = block_ranks(keys)
    return placed([(keys, values)], [rank & (SUBS - 1)], [rank >> 3], SUBS)


HALF = SUBS // 2
TALL = SUBS + HALF
SHIFT = BIG // 2
AXIS = 4


def hops(offset):
    return sum(min(k, AXIS - k) for k in offset)


OFFSETS = sorted(((dx, dz, dy) for dx in range(AXIS) for dz in range(AXIS) for dy in range(AXIS)), key=lambda o: -hops(o))


def gather_kernel(
    keys_ref,
    values_ref,
    found_ref,
    sample,
    block,
    rows,
    blocks,
    turns,
    inside,
    row_send,
    row_recv,
    send_sem,
    recv_sem,
    give_sem,
    take_sem,
):
    gx, gy = lax.axis_index("gx"), lax.axis_index("gy")
    x, core, z, y = gx // 2, gx % 2, gy // AXIS, gy % AXIS
    planes = AXIS * AXIS
    devices = 2 * AXIS * planes
    me = gx * planes + gy
    barrier = pltpu.get_barrier_semaphore()

    def device(offset, other):
        dx, dz, dy = offset
        which = 1 - core if other else core
        return ((x + dx) % AXIS) * 2 + which, ((z + dz) % AXIS) * AXIS + (y + dy) % AXIS

    peers = [(o, device(o, other), other) for o in OFFSETS for other in (1, 0) if other or hops(o)]
    for _, peer, _ in peers:
        pl.semaphore_signal(barrier, inc=1, device_id=peer, device_id_type=MESH)

    keys, values = sorted_block(keys_ref[...], values_ref[...])
    for ref in (sample, rows.at[me]):
        ref[...] = keys[SUBS - 1 :, :]
    for ref in (block, blocks.at[me]):
        ref[:SUBS, :] = ((keys - SHIFT) << 8) | (values >> 16)
        ref[SUBS:, :] = (values[:HALF, :] & 0xFFFF) | (values[HALF:, :] << 16)
    pl.semaphore_wait(barrier, devices - 1)

    for _, peer, _ in peers:
        pltpu.make_async_remote_copy(
            src_ref=sample,
            dst_ref=rows.at[me],
            send_sem=row_send,
            recv_sem=row_recv,
            device_id=peer,
            device_id_type=MESH,
        ).start()
    for (dx, dz, dy), peer, other in peers:
        if not other:
            pltpu.make_async_remote_copy(
                src_ref=block,
                dst_ref=blocks.at[me],
                send_sem=send_sem,
                recv_sem=recv_sem.at[(AXIS - dx) % AXIS],
                device_id=peer,
                device_id_type=MESH,
            ).start()

    all_rows = rows.at[pl.ds(0, devices - 1)]
    pltpu.make_async_copy(all_rows, all_rows, row_recv).wait()
    wanted = [me * LANES, (me + 1) * LANES]
    found = [jnp.zeros((SUBS, LANES), i32)] * 2
    found = search(rows, wanted, found, SHIFTS[:EARLY])
    gives = []
    for dx in (0, 1, 3, 2):
        at = (((x + dx) % AXIS) * 2 + core) * planes
        arrived = blocks.at[pl.ds(at, planes if dx else planes - 1)]
        pltpu.make_async_copy(arrived, arrived, recv_sem.at[dx]).wait()
        group = blocks.at[pl.ds(at, planes)]
        give = pltpu.make_async_remote_copy(
            src_ref=group,
            dst_ref=group,
            send_sem=give_sem.at[dx],
            recv_sem=take_sem.at[dx],
            device_id=(x * 2 + 1 - core, gy),
            device_id_type=MESH,
        )
        give.start()
        gives.append(give)
    low, high = search(rows, wanted, found, SHIFTS[EARLY:])
    high = jnp.where(me == devices - 1, BIG, high)
    codes = group_plan(wanted, low, high, rows, turns, inside)
    tiles = [jnp.zeros((SUBS, LANES), i32)] * 4
    tiles = collect(tiles, blocks, turns, inside, core)
    for give in gives:
        give.wait_recv()
    tiles = collect(tiles, blocks, turns, inside, 1 - core)
    keys, values = unpacked(tiles, codes, low, high)
    for n, tile in enumerate(keys + values):
        found_ref[n * SUBS : (n + 1) * SUBS, :] = tile
    pltpu.make_async_copy(all_rows, all_rows, row_send).wait()
    sent = blocks.at[pl.ds(0, AXIS * planes - 1)]
    pltpu.make_async_copy(sent, sent, send_sem).wait()
    for give in gives:
        give.wait_send()


SHIFTS = tuple(range(21, -1, -3))
EARLY = 4


def search(rows_ref, wanted, base, shifts):
    subs = iota((SUBS, LANES), 0)
    base = list(base)
    zero = jnp.zeros((SUBS, LANES), i32)
    for shift in shifts:
        tests = [b + ((subs + 1) << shift) for b in base]
        accs = [[zero, zero] for _ in tests]
        for r in range(LANES):
            one = jnp.broadcast_to(rows_ref[r], (SUBS, LANES))
            for n, test in enumerate(tests):
                accs[n][r % 2] = accs[n][r % 2] + jnp.where(one < test, 1, 0)
        for n in range(len(wanted)):
            below = jnp.sum((accs[n][0] + accs[n][1]).astype(f32), axis=1, keepdims=True)
            passed = jnp.where((below < wanted[n].astype(f32)) & (subs[:, :1] < SUBS - 1), 1, 0)
            digit = jnp.sum(passed, axis=0, keepdims=True)
            base[n] = base[n] + (jnp.broadcast_to(digit, (SUBS, LANES)) << shift)
    return base


def group_plan(wanted, low, high, rows_ref, turn_ref, in_ref):
    square = (LANES, LANES)
    samples = rows_ref[...].reshape(square)
    ends = [jnp.broadcast_to(k[:1, :], square) for k in (low, high)]
    ones = jnp.ones(square, bf16)
    below = jnp.where(iota(square, 1) < iota(square, 0), 1.0, 0.0).astype(bf16)

    def mm(a, b):
        return jnp.dot(a, b, preferred_element_type=f32)

    masks = []
    for k in ends:
        masks += [samples < k, samples <= k]
    counts = mm(jnp.concatenate([jnp.where(m, 1.0, 0.0).astype(bf16) for m in masks], axis=0), ones)
    counts = [counts[n * LANES : (n + 1) * LANES, :] for n in range(4)]
    taken, tied = [], []
    for n in range(2):
        lt, le = counts[2 * n], counts[2 * n + 1]
        equal = le - lt
        before = mm(below, equal.astype(bf16))
        total = mm(ones, lt.astype(bf16))
        left = jnp.asarray(wanted[n], f32) - total - before
        taken.append(lt + jnp.clip(left, 0.0, equal))
        tied.append(jnp.where(left > equal, 1, 0))
    first = taken[0]
    number = jnp.minimum(taken[1], LANES - 1.0) - first + 1.0
    start = mm(below, number.astype(bf16)).astype(i32)
    number, first, last = number.astype(i32), first.astype(i32), taken[1].astype(i32)
    lanes = iota(square, 1)
    turn_ref[...] = (lanes - (start - first)) & (LANES - 1)
    codes = []
    for h in range(2):
        m = lanes + h * LANES
        inside = (m >= start) & (m < start + number)
        in_ref[h] = jnp.where(inside, 1, 0)
        code = jnp.where(inside, 16, 0)
        code = code + jnp.where(inside & (m == start), 1 + tied[0], 0)
        code = code + jnp.where(inside & (m == start + last - first), 4 * (1 + tied[1]), 0)
        codes.append(code.astype(f32).astype(bf16))
    return mm(jnp.ones((SUBS, LANES), bf16), jnp.concatenate(codes, axis=1)).astype(i32)


def collect(tiles, blocks_ref, turn_ref, in_ref, core):
    tiles = list(tiles)
    planes = AXIS * AXIS
    for at in range(AXIS * planes):
        b = (at // planes * 2 + core) * planes + at % planes
        turn = jnp.broadcast_to(turn_ref[pl.ds(b, 1), :], (SUBS, LANES))
        rest = blocks_ref[b, SUBS:, :]
        for c, tile in enumerate((blocks_ref[b, :SUBS, :], jnp.concatenate([rest, rest], axis=0))):
            tile = jnp.take_along_axis(tile, turn, axis=1, mode="promise_in_bounds")
            for h in range(2):
                inside = jnp.broadcast_to(in_ref[h, pl.ds(b, 1), :], (SUBS, LANES)) > 0
                tiles[2 * c + h] = jnp.where(inside, tile, tiles[2 * c + h])
    return tiles


def unpacked(tiles, codes, low, high):
    upper = iota((SUBS, LANES), 0) >= HALF
    keys, values = [], []
    for h in range(2):
        w, r = tiles[h], tiles[2 + h]
        k = (w >> 8) + SHIFT
        values.append(((w & 255) << 16) | (jnp.where(upper, r >> 16, r) & 0xFFFF))
        code = codes[:, h * LANES : (h + 1) * LANES]
        is_low, is_high = code & 3, (code >> 2) & 3
        ok = code >= 16
        ok = ok & ((is_low == 0) | (k >= low + is_low - 1))
        ok = ok & ((is_high == 0) | (k < high + is_high - 1))
        keys.append(jnp.where(ok, k, BIG))
    return keys, values


def place_kernel(found_ref, keys_out, values_out, size_out, digest_out):
    found = [found_ref[n * SUBS : (n + 1) * SUBS, :] for n in range(4)]
    keys, values = found[:2], found[2:]
    valid = jnp.where(keys[0] < BIG, 1, 0) + jnp.where(keys[1] < BIG, 1, 0)
    size = jnp.sum(jnp.sum(valid, axis=1, keepdims=True), axis=0, keepdims=True)
    ranks = candidate_ranks(keys)
    count = 2 * SUBS
    keys, values = placed(
        list(zip(keys, values)), [r >> 7 for r in ranks], [r & (LANES - 1) for r in ranks], count
    )
    rank = iota((count, LANES), 0) * LANES + iota((count, LANES), 1)
    filled = rank < size
    keys = jnp.where(filled, keys, -1)
    values = jnp.where(filled, values, -1)
    keys_out[...] = keys[: keys_out.shape[0], :]
    values_out[...] = values[: values_out.shape[0], :]
    mixed = (keys + 3 * values + 5 * rank) & 1023
    digest = jnp.where(filled, 2 * mixed - 1023, 0)
    digest = jnp.sum(jnp.sum(digest, axis=1, keepdims=True), axis=0, keepdims=True)
    size_out[0] = size[0, 0]
    digest_out[0] = digest[0, 0]


def candidates(keys, values):
    dma = pltpu.SemaphoreType.DMA
    return pl.pallas_call(
        gather_kernel,
        out_shape=jax.ShapeDtypeStruct((4 * SUBS, LANES), i32),
        in_specs=[pl.BlockSpec(memory_space=pltpu.VMEM)] * 2,
        out_specs=pl.BlockSpec(memory_space=pltpu.VMEM),
        scratch_shapes=[
            pltpu.VMEM((1, LANES), i32),
            pltpu.VMEM((TALL, LANES), i32),
            pltpu.VMEM((LANES, 1, LANES), i32),
            pltpu.VMEM((LANES, TALL, LANES), i32),
            pltpu.VMEM((LANES, LANES), i32),
            pltpu.VMEM((2, LANES, LANES), i32),
            dma,
            dma,
            dma,
            dma((AXIS,)),
            dma((AXIS,)),
            dma((AXIS,)),
        ],
        compiler_params=pltpu.CompilerParams(collective_id=0, has_side_effects=True),
        name="find_candidates",
    )(keys, values)


def placed_bucket(found, rows):
    one = jax.ShapeDtypeStruct((1,), i32)
    return pl.pallas_call(
        place_kernel,
        out_shape=(jax.ShapeDtypeStruct((rows, LANES), i32),) * 2 + (one, one),
        in_specs=[pl.BlockSpec(memory_space=pltpu.VMEM)],
        out_specs=[pl.BlockSpec(memory_space=pltpu.VMEM)] * 2 + [pl.BlockSpec(memory_space=pltpu.SMEM)] * 2,
        name="place_bucket",
    )(found)


def solution(mesh):
    gx, gy = mesh.shape["gx"], mesh.shape["gy"]

    def shards(record_keys, payloads):
        keys = record_keys.reshape(SUBS, LANES)
        values = payloads.reshape(SUBS, LANES)
        found = candidates(keys, values)
        rows = (2 * record_keys.shape[0] - gx * gy) // LANES
        sorted_keys, sorted_values, size, digest = placed_bucket(found, rows)
        return sorted_keys.reshape(-1), sorted_values.reshape(-1), size, digest

    spec = P(("gx", "gy"))
    return jax.shard_map(shards, mesh=mesh, in_specs=(spec,) * 2, out_specs=(spec,) * 4, check_vma=False)
```

time: 31.7 us -> 27.1 us (0.85)
  Pallas kernels: 30.8 us -> 26.2 us
    pallas_call x1, Pallas kernels: 26.1 us -> 22.7 us  [candidates(): pl.pallas_call(gather_kernel, out_shape=jax.ShapeDtypeStruct((4 * SUBS, L...]
    pallas_call x1, Pallas kernels: 4.71 us -> 3.51 us  [placed_bucket(): pl.pallas_call(place_kernel, out_shape=(jax.ShapeDtypeStruct((rows, LANES...]
where the time goes in v3:
time: 27.1 us; the launch traced here: 26.8 us
  Pallas kernels  26.2 us (97%)
  between operations  0.64 us (2%)
    pallas_call x1, Pallas kernels, candidates(): pl.pallas_call(gather_kernel, out_shape=jax.ShapeDtypeStruct((4 * SUBS, L...  22.7 us
    pallas_call x1, Pallas kernels, placed_bucket(): pl.pallas_call(place_kernel, out_shape=(jax.ShapeDtypeStruct((rows, LANES...  3.51 us

profile of v3, /device:TPU:1, one launch (start us, length us, event | category | flops | bytes accessed | tf_op | source)
XLA Modules:
  0.0 26.8 jit_solution(12733128281529492894)
XLA Ops:
  0.6 22.7 %find_candidates.1.found_ref = s32[32,128]{1,0:T(8,128)} custom-call(s32[8,128]{1,0:T(8,128)} %bitcast.4, s32[8,128]{1,0:T(8,128)} %bitcast.5), custom_call_target="tpu_custom_call" | custom-call | tf_op jit(solution)/shard_map/find_candidates/pallas_call | solution.py:338
  23.3 3.5 %place_bucket.1 = (s32[15,128]{1,0:T(8,128)}, s32[15,128]{1,0:T(8,128)}, s32[1]{0:T(128)}, s32[1]{0:T(128)}) custom-call(s32[32,128]{1,0:T(8,128)} %find_candidates.1.found_ref), custom_call_target="tpu_custom_call" | custom-call | tf_op jit(solution)/shard_map/place_bucket/pallas_call | solution.py:364

commit v4 on v3

--- a/solution.py
+++ b/solution.py
@@ -101,10 +101,20 @@
     return placed([(keys, values)], [rank & (SUBS - 1)], [rank >> 3], SUBS)
 
 
-HALF = SUBS // 2
-TALL = SUBS + HALF
-SHIFT = BIG // 2
+SHORT = 6
+BYTE = 24
 AXIS = 4
+
+
+def packed(x):
+    extra = [(x[SHORT + r // 3 : SHORT + r // 3 + 1, :] >> (8 * (r % 3))) & 255 for r in range(SHORT)]
+    return x[:SHORT, :] | (jnp.concatenate(extra, axis=0) << BYTE)
+
+
+def unpacked(x):
+    extra = (x >> BYTE) & 255
+    last = [extra[r : r + 1, :] | (extra[r + 1 : r + 2, :] << 8) | (extra[r + 2 : r + 3, :] << 16) for r in (0, 3)]
+    return jnp.concatenate([x[:SHORT, :] & (BIG - 1)] + last, axis=0)
 
 
 def hops(offset):
@@ -115,15 +125,17 @@
 
 
 def gather_kernel(
-    keys_ref,
-    values_ref,
+    keys_hbm,
+    values_hbm,
     found_ref,
+    local,
     sample,
     block,
     rows,
     blocks,
     turns,
     inside,
+    local_sem,
     row_send,
     row_recv,
     send_sem,
@@ -137,6 +149,9 @@
     devices = 2 * AXIS * planes
     me = gx * planes + gy
     barrier = pltpu.get_barrier_semaphore()
+    loads = [pltpu.make_async_copy(ref, local.at[c], local_sem.at[c]) for c, ref in enumerate((keys_hbm, values_hbm))]
+    for load in loads:
+        load.start()
 
     def device(offset, other):
         dx, dz, dy = offset
@@ -146,13 +161,16 @@
     peers = [(o, device(o, other), other) for o in OFFSETS for other in (1, 0) if other or hops(o)]
     for _, peer, _ in peers:
         pl.semaphore_signal(barrier, inc=1, device_id=peer, device_id_type=MESH)
-
-    keys, values = sorted_block(keys_ref[...], values_ref[...])
+    for load in loads:
+        load.wait()
+
+    keys, values = sorted_block(local[0], local[1])
     for ref in (sample, rows.at[me]):
         ref[...] = keys[SUBS - 1 :, :]
-    for ref in (block, blocks.at[me]):
-        ref[:SUBS, :] = ((keys - SHIFT) << 8) | (values >> 16)
-        ref[SUBS:, :] = (values[:HALF, :] & 0xFFFF) | (values[HALF:, :] << 16)
+    for c, tile in enumerate((keys, values)):
+        tile = packed(tile)
+        block[c] = tile
+        blocks[c, me] = tile
     pl.semaphore_wait(barrier, devices - 1)
 
     for _, peer, _ in peers:
@@ -164,53 +182,64 @@
             device_id=peer,
             device_id_type=MESH,
         ).start()
-    for (dx, dz, dy), peer, other in peers:
-        if not other:
-            pltpu.make_async_remote_copy(
-                src_ref=block,
-                dst_ref=blocks.at[me],
-                send_sem=send_sem,
-                recv_sem=recv_sem.at[(AXIS - dx) % AXIS],
-                device_id=peer,
+    for c in range(2):
+        for (dx, dz, dy), peer, other in peers:
+            if not other:
+                pltpu.make_async_remote_copy(
+                    src_ref=block.at[c],
+                    dst_ref=blocks.at[c, me],
+                    send_sem=send_sem.at[c],
+                    recv_sem=recv_sem.at[c, (AXIS - dx) % AXIS],
+                    device_id=peer,
+                    device_id_type=MESH,
+                ).start()
+
+    def forward(c):
+        gives = []
+        for dx in (0, 1, 3, 2):
+            at = (((x + dx) % AXIS) * 2 + core) * planes
+            arrived = blocks.at[c, pl.ds(at, planes if dx else planes - 1)]
+            pltpu.make_async_copy(arrived, arrived, recv_sem.at[c, dx]).wait()
+            group = blocks.at[c, pl.ds(at, planes)]
+            give = pltpu.make_async_remote_copy(
+                src_ref=group,
+                dst_ref=group,
+                send_sem=give_sem.at[c, dx],
+                recv_sem=take_sem.at[c, dx],
+                device_id=(x * 2 + 1 - core, gy),
                 device_id_type=MESH,
-            ).start()
+            )
+            give.start()
+            gives.append(give)
+        return gives
 
     all_rows = rows.at[pl.ds(0, devices - 1)]
     pltpu.make_async_copy(all_rows, all_rows, row_recv).wait()
     wanted = [me * LANES, (me + 1) * LANES]
-    found = [jnp.zeros((SUBS, LANES), i32)] * 2
-    found = search(rows, wanted, found, SHIFTS[:EARLY])
-    gives = []
-    for dx in (0, 1, 3, 2):
-        at = (((x + dx) % AXIS) * 2 + core) * planes
-        arrived = blocks.at[pl.ds(at, planes if dx else planes - 1)]
-        pltpu.make_async_copy(arrived, arrived, recv_sem.at[dx]).wait()
-        group = blocks.at[pl.ds(at, planes)]
-        give = pltpu.make_async_remote_copy(
-            src_ref=group,
-            dst_ref=group,
-            send_sem=give_sem.at[dx],
-            recv_sem=take_sem.at[dx],
-            device_id=(x * 2 + 1 - core, gy),
-            device_id_type=MESH,
-        )
-        give.start()
-        gives.append(give)
-    low, high = search(rows, wanted, found, SHIFTS[EARLY:])
+    zero = jnp.zeros((SUBS, LANES), i32)
+    ends = search(rows, wanted, [zero] * 2, SHIFTS[:EARLY])
+    key_gives = forward(0)
+    low, high = search(rows, wanted, ends, SHIFTS[EARLY:])
     high = jnp.where(me == devices - 1, BIG, high)
     codes = group_plan(wanted, low, high, rows, turns, inside)
-    tiles = [jnp.zeros((SUBS, LANES), i32)] * 4
-    tiles = collect(tiles, blocks, turns, inside, core)
-    for give in gives:
+    tiles = collect([zero] * 2, blocks, 0, turns, inside, core)
+    value_gives = forward(1)
+    for give in key_gives:
         give.wait_recv()
-    tiles = collect(tiles, blocks, turns, inside, 1 - core)
-    keys, values = unpacked(tiles, codes, low, high)
-    for n, tile in enumerate(keys + values):
+    tiles = collect(tiles, blocks, 0, turns, inside, 1 - core)
+    keys = bucket_keys(tiles, codes, low, high)
+    ranks = candidate_ranks(keys)
+    tiles = collect([zero] * 2, blocks, 1, turns, inside, core)
+    for give in value_gives:
+        give.wait_recv()
+    tiles = collect(tiles, blocks, 1, turns, inside, 1 - core)
+    for n, tile in enumerate(keys + [unpacked(t) for t in tiles] + ranks):
         found_ref[n * SUBS : (n + 1) * SUBS, :] = tile
     pltpu.make_async_copy(all_rows, all_rows, row_send).wait()
-    sent = blocks.at[pl.ds(0, AXIS * planes - 1)]
-    pltpu.make_async_copy(sent, sent, send_sem).wait()
-    for give in gives:
+    for c in range(2):
+        sent = blocks.at[c, pl.ds(0, AXIS * planes - 1)]
+        pltpu.make_async_copy(sent, sent, send_sem.at[c]).wait()
+    for give in key_gives + value_gives:
         give.wait_send()
 
 
@@ -279,43 +308,39 @@
     return mm(jnp.ones((SUBS, LANES), bf16), jnp.concatenate(codes, axis=1)).astype(i32)
 
 
-def collect(tiles, blocks_ref, turn_ref, in_ref, core):
+def collect(tiles, blocks_ref, c, turn_ref, in_ref, core):
     tiles = list(tiles)
     planes = AXIS * AXIS
+    empty = jnp.zeros((SUBS - SHORT, LANES), i32)
     for at in range(AXIS * planes):
         b = (at // planes * 2 + core) * planes + at % planes
         turn = jnp.broadcast_to(turn_ref[pl.ds(b, 1), :], (SUBS, LANES))
-        rest = blocks_ref[b, SUBS:, :]
-        for c, tile in enumerate((blocks_ref[b, :SUBS, :], jnp.concatenate([rest, rest], axis=0))):
-            tile = jnp.take_along_axis(tile, turn, axis=1, mode="promise_in_bounds")
-            for h in range(2):
-                inside = jnp.broadcast_to(in_ref[h, pl.ds(b, 1), :], (SUBS, LANES)) > 0
-                tiles[2 * c + h] = jnp.where(inside, tile, tiles[2 * c + h])
+        tile = jnp.concatenate([blocks_ref[c, b], empty], axis=0)
+        tile = jnp.take_along_axis(tile, turn, axis=1, mode="promise_in_bounds")
+        for h in range(2):
+            here = jnp.broadcast_to(in_ref[h, pl.ds(b, 1), :], (SUBS, LANES)) > 0
+            tiles[h] = jnp.where(here, tile, tiles[h])
     return tiles
 
 
-def unpacked(tiles, codes, low, high):
-    upper = iota((SUBS, LANES), 0) >= HALF
-    keys, values = [], []
-    for h in range(2):
-        w, r = tiles[h], tiles[2 + h]
-        k = (w >> 8) + SHIFT
-        values.append(((w & 255) << 16) | (jnp.where(upper, r >> 16, r) & 0xFFFF))
+def bucket_keys(tiles, codes, low, high):
+    keys = []
+    for h, tile in enumerate(tiles):
+        k = unpacked(tile)
         code = codes[:, h * LANES : (h + 1) * LANES]
         is_low, is_high = code & 3, (code >> 2) & 3
         ok = code >= 16
         ok = ok & ((is_low == 0) | (k >= low + is_low - 1))
         ok = ok & ((is_high == 0) | (k < high + is_high - 1))
         keys.append(jnp.where(ok, k, BIG))
-    return keys, values
+    return keys
 
 
 def place_kernel(found_ref, keys_out, values_out, size_out, digest_out):
-    found = [found_ref[n * SUBS : (n + 1) * SUBS, :] for n in range(4)]
-    keys, values = found[:2], found[2:]
+    found = [found_ref[n * SUBS : (n + 1) * SUBS, :] for n in range(6)]
+    keys, values, ranks = found[:2], found[2:4], found[4:]
     valid = jnp.where(keys[0] < BIG, 1, 0) + jnp.where(keys[1] < BIG, 1, 0)
     size = jnp.sum(jnp.sum(valid, axis=1, keepdims=True), axis=0, keepdims=True)
-    ranks = candidate_ranks(keys)
     count = 2 * SUBS
     keys, values = placed(
         list(zip(keys, values)), [r >> 7 for r in ranks], [r & (LANES - 1) for r in ranks], count
@@ -337,22 +362,24 @@
     dma = pltpu.SemaphoreType.DMA
     return pl.pallas_call(
         gather_kernel,
-        out_shape=jax.ShapeDtypeStruct((4 * SUBS, LANES), i32),
-        in_specs=[pl.BlockSpec(memory_space=pltpu.VMEM)] * 2,
+        out_shape=jax.ShapeDtypeStruct((6 * SUBS, LANES), i32),
+        in_specs=[pl.BlockSpec(memory_space=pltpu.HBM)] * 2,
         out_specs=pl.BlockSpec(memory_space=pltpu.VMEM),
         scratch_shapes=[
+            pltpu.VMEM((2, SUBS, LANES), i32),
             pltpu.VMEM((1, LANES), i32),
-            pltpu.VMEM((TALL, LANES), i32),
+            pltpu.VMEM((2, SHORT, LANES), i32),
             pltpu.VMEM((LANES, 1, LANES), i32),
-            pltpu.VMEM((LANES, TALL, LANES), i32),
+            pltpu.VMEM((2, LANES, SHORT, LANES), i32),
             pltpu.VMEM((LANES, LANES), i32),
             pltpu.VMEM((2, LANES, LANES), i32),
+            dma((2,)),
             dma,
             dma,
-            dma,
-            dma((AXIS,)),
-            dma((AXIS,)),
-            dma((AXIS,)),
+            dma((2,)),
+            dma((2, AXIS)),
+            dma((2, AXIS)),
+            dma((2, AXIS)),
         ],
         compiler_params=pltpu.CompilerParams(collective_id=0, has_side_effects=True),
         name="find_candidates",

time: 27.1 us -> 24.4 us (0.900)
  Pallas kernels: 26.2 us -> 23.6 us
    pallas_call x1, Pallas kernels: 3.51 us -> 1.7 us  [placed_bucket(): pl.pallas_call(place_kernel, out_shape=(jax.ShapeDtypeStruct((rows, LANES...]
    pallas_call x1, Pallas kernels: 22.7 us -> 21.9 us  [candidates(): pl.pallas_call(gather_kernel, out_shape=jax.ShapeDtypeStruct((6 * SUBS, L...]
where the time goes in v4:
time: 24.4 us; the launch traced here: 24.3 us
  Pallas kernels  23.6 us (97%)
  between operations  0.64 us (3%)
    pallas_call x1, Pallas kernels, candidates(): pl.pallas_call(gather_kernel, out_shape=jax.ShapeDtypeStruct((6 * SUBS, L...  21.9 us
    pallas_call x1, Pallas kernels, placed_bucket(): pl.pallas_call(place_kernel, out_shape=(jax.ShapeDtypeStruct((rows, LANES...  1.7 us

profile of v4, /device:TPU:1, one launch (start us, length us, event | category | flops | bytes accessed | tf_op | source)
XLA Modules:
  0.0 24.3 jit_solution(1621702371152800902)
XLA Ops:
  0.6 21.9 %find_candidates.1.found_ref = s32[48,128]{1,0:T(8,128)} custom-call(s32[8,128]{1,0:T(8,128)} %bitcast.4, s32[8,128]{1,0:T(8,128)} %bitcast.5), custom_call_target="tpu_custom_call" | custom-call | tf_op jit(solution)/shard_map/find_candidates/pallas_call | solution.py:363
  22.6 1.7 %place_bucket.1 = (s32[15,128]{1,0:T(8,128)}, s32[15,128]{1,0:T(8,128)}, s32[1]{0:T(128)}, s32[1]{0:T(128)}) custom-call(s32[48,128]{1,0:T(8,128)} %find_candidates.1.found_ref), custom_call_target="tpu_custom_call" | custom-call | tf_op jit(solution)/shard_map/place_bucket/pallas_call | solution.py:391

commit v5 on v4

--- a/solution.py
+++ b/solution.py
@@ -381,7 +381,7 @@
             dma((2, AXIS)),
             dma((2, AXIS)),
         ],
-        compiler_params=pltpu.CompilerParams(collective_id=0, has_side_effects=True),
+        compiler_params=pltpu.CompilerParams(collective_id=0, has_side_effects=True, vmem_limit_bytes=8 << 20),
         name="find_candidates",
     )(keys, values)
 
@@ -393,6 +393,7 @@
         out_shape=(jax.ShapeDtypeStruct((rows, LANES), i32),) * 2 + (one, one),
         in_specs=[pl.BlockSpec(memory_space=pltpu.VMEM)],
         out_specs=[pl.BlockSpec(memory_space=pltpu.VMEM)] * 2 + [pl.BlockSpec(memory_space=pltpu.SMEM)] * 2,
+        compiler_params=pltpu.CompilerParams(vmem_limit_bytes=8 << 20),
         name="place_bucket",
     )(found)
 
@@ -403,6 +404,7 @@
     def shards(record_keys, payloads):
         keys = record_keys.reshape(SUBS, LANES)
         values = payloads.reshape(SUBS, LANES)
+        keys, values = (pltpu.with_memory_space_constraint(a, pltpu.HBM) for a in (keys, values))
         found = candidates(keys, values)
         rows = (2 * record_keys.shape[0] - gx * gy) // LANES
         sorted_keys, sorted_values, size, digest = placed_bucket(found, rows)

time: 24.4 us -> 23 us (0.943)
  Pallas kernels: 23.6 us -> 22.3 us
    pallas_call x1, Pallas kernels: 1.7 us -> 0.96 us  [placed_bucket(): pl.pallas_call(place_kernel, out_shape=(jax.ShapeDtypeStruct((rows, LANES...]
    pallas_call x1, Pallas kernels: 21.9 us -> 21.3 us  [candidates(): pl.pallas_call(gather_kernel, out_shape=jax.ShapeDtypeStruct((6 * SUBS, L...]
where the time goes in v5:
time: 23 us; the launch traced here: 22.9 us
  Pallas kernels  22.3 us (97%)
  between operations  0.64 us (3%)
    pallas_call x1, Pallas kernels, candidates(): pl.pallas_call(gather_kernel, out_shape=jax.ShapeDtypeStruct((6 * SUBS, L...  21.3 us
    pallas_call x1, Pallas kernels, placed_bucket(): pl.pallas_call(place_kernel, out_shape=(jax.ShapeDtypeStruct((rows, LANES...  0.96 us

profile of v5, /device:TPU:1, one launch (start us, length us, event | category | flops | bytes accessed | tf_op | source)
XLA Modules:
  0.0 22.9 jit_solution(3723273072551878163)
XLA Ops:
  0.6 21.3 %find_candidates.1.found_ref = s32[48,128]{1,0:T(8,128)S(1)} custom-call(s32[8,128]{1,0:T(8,128)} %bitcast.4, s32[8,128]{1,0:T(8,128)} %bitcast.5), custom_call_target="tpu_custom_call" | custom-call | tf_op jit(solution)/shard_map/find_candidates/pallas_call | solution.py:363
  21.9 1.0 %place_bucket.1 = (s32[15,128]{1,0:T(8,128)}, s32[15,128]{1,0:T(8,128)}, s32[1]{0:T(128)}, s32[1]{0:T(128)}) custom-call(s32[48,128]{1,0:T(8,128)S(1)} %find_candidates.1.found_ref), custom_call_target="tpu_custom_call" | custom-call | tf_op jit(solution)/shard_map/place_bucket/pallas_call | solution.py:391

commit v6 on v5

--- a/solution.py
+++ b/solution.py
@@ -76,23 +76,35 @@
 def candidate_ranks(halves):
     subs, lanes = iota((SUBS, LANES), 0), iota((SUBS, LANES), 1)
     zero = jnp.zeros((SUBS, LANES), i32)
+    width = LANES // SUBS
+    spread = (lanes + width * subs) & (LANES - 1)
+    tables = [
+        [jnp.take_along_axis(row(k, s), spread, axis=1, mode="promise_in_bounds") for s in range(SUBS)] for k in halves
+    ]
+    dropped = sum(jnp.where(k < 0, 1, 0) for k in halves)
+    dropped = jnp.sum(jnp.sum(dropped, axis=1, keepdims=True), axis=0, keepdims=True)
     ranks = []
     for target, keys in enumerate(halves):
         rows = [row(keys, s) for s in range(SUBS)]
         accs = [zero] * SUBS
-        for source, others in enumerate(halves):
+        for source, table in enumerate(tables):
             if target > source:
-                others = others - 1
-            for m in range(LANES):
-                one = column(others, m)
+                table = [t - 1 for t in table]
+            for m in range(width):
+                ones = [column(t, m) for t in table]
                 if target == source:
-                    one = one - jnp.where(lanes > m, 1, 0)
-                for s in range(SUBS):
-                    accs[s] = accs[s] + jnp.where(one < rows[s], 1, 0)
+                    after = jnp.where(lanes > m + width * subs, 1, 0)
+                    ones = [one - after for one in ones]
+                for r in range(SUBS):
+                    count = jnp.where(ones[0] < rows[r], 1, 0)
+                    for s in range(1, SUBS):
+                        count = jnp.where(ones[s] < rows[r], s + 1, count)
+                    accs[r] = accs[r] + count
         ties = zero
         for d in range(1, SUBS):
             ties = ties + jnp.where((pltpu.roll(keys, d, 0) == keys) & (subs >= d), 1, 0)
-        ranks.append(sublane_sums(accs) + ties)
+        rank = sublane_sums(accs) + ties - dropped
+        ranks.append(jnp.where((keys >= 0) & (keys < BIG), rank, 2 * SUBS * LANES - 1))
     return ranks
 
 
@@ -138,6 +150,8 @@
     local_sem,
     row_send,
     row_recv,
+    row_give,
+    row_take,
     send_sem,
     recv_sem,
     give_sem,
@@ -153,13 +167,13 @@
     for load in loads:
         load.start()
 
-    def device(offset, other):
+    def device(offset):
         dx, dz, dy = offset
-        which = 1 - core if other else core
-        return ((x + dx) % AXIS) * 2 + which, ((z + dz) % AXIS) * AXIS + (y + dy) % AXIS
-
-    peers = [(o, device(o, other), other) for o in OFFSETS for other in (1, 0) if other or hops(o)]
-    for _, peer, _ in peers:
+        return ((x + dx) % AXIS) * 2 + core, ((z + dz) % AXIS) * AXIS + (y + dy) % AXIS
+
+    peers = [(o, device(o)) for o in OFFSETS if hops(o)]
+    partner = (x * 2 + 1 - core, gy)
+    for _, peer in peers + [(None, partner)]:
         pl.semaphore_signal(barrier, inc=1, device_id=peer, device_id_type=MESH)
     for load in loads:
         load.wait()
@@ -171,9 +185,9 @@
         tile = packed(tile)
         block[c] = tile
         blocks[c, me] = tile
-    pl.semaphore_wait(barrier, devices - 1)
-
-    for _, peer, _ in peers:
+    pl.semaphore_wait(barrier, AXIS * planes)
+
+    for _, peer in peers:
         pltpu.make_async_remote_copy(
             src_ref=sample,
             dst_ref=rows.at[me],
@@ -183,16 +197,15 @@
             device_id_type=MESH,
         ).start()
     for c in range(2):
-        for (dx, dz, dy), peer, other in peers:
-            if not other:
-                pltpu.make_async_remote_copy(
-                    src_ref=block.at[c],
-                    dst_ref=blocks.at[c, me],
-                    send_sem=send_sem.at[c],
-                    recv_sem=recv_sem.at[c, (AXIS - dx) % AXIS],
-                    device_id=peer,
-                    device_id_type=MESH,
-                ).start()
+        for (dx, dz, dy), peer in peers:
+            pltpu.make_async_remote_copy(
+                src_ref=block.at[c],
+                dst_ref=blocks.at[c, me],
+                send_sem=send_sem.at[c],
+                recv_sem=recv_sem.at[c, (AXIS - dx) % AXIS],
+                device_id=peer,
+                device_id_type=MESH,
+            ).start()
 
     def forward(c):
         gives = []
@@ -206,15 +219,27 @@
                 dst_ref=group,
                 send_sem=give_sem.at[c, dx],
                 recv_sem=take_sem.at[c, dx],
-                device_id=(x * 2 + 1 - core, gy),
+                device_id=partner,
                 device_id_type=MESH,
             )
             give.start()
             gives.append(give)
         return gives
 
-    all_rows = rows.at[pl.ds(0, devices - 1)]
-    pltpu.make_async_copy(all_rows, all_rows, row_recv).wait()
+    some_rows = rows.at[pl.ds(0, AXIS * planes - 1)]
+    pltpu.make_async_copy(some_rows, some_rows, row_recv).wait()
+    for dx in range(AXIS):
+        group = rows.at[pl.ds(((x + dx) % AXIS * 2 + core) * planes, planes)]
+        pltpu.make_async_remote_copy(
+            src_ref=group,
+            dst_ref=group,
+            send_sem=row_give,
+            recv_sem=row_take,
+            device_id=partner,
+            device_id_type=MESH,
+        ).start()
+    half_rows = rows.at[pl.ds(0, AXIS * planes)]
+    pltpu.make_async_copy(half_rows, half_rows, row_take).wait()
     wanted = [me * LANES, (me + 1) * LANES]
     zero = jnp.zeros((SUBS, LANES), i32)
     ends = search(rows, wanted, [zero] * 2, SHIFTS[:EARLY])
@@ -235,7 +260,8 @@
     tiles = collect(tiles, blocks, 1, turns, inside, 1 - core)
     for n, tile in enumerate(keys + [unpacked(t) for t in tiles] + ranks):
         found_ref[n * SUBS : (n + 1) * SUBS, :] = tile
-    pltpu.make_async_copy(all_rows, all_rows, row_send).wait()
+    pltpu.make_async_copy(some_rows, some_rows, row_send).wait()
+    pltpu.make_async_copy(half_rows, half_rows, row_give).wait()
     for c in range(2):
         sent = blocks.at[c, pl.ds(0, AXIS * planes - 1)]
         pltpu.make_async_copy(sent, sent, send_sem.at[c]).wait()
@@ -259,10 +285,11 @@
             for n, test in enumerate(tests):
                 accs[n][r % 2] = accs[n][r % 2] + jnp.where(one < test, 1, 0)
         for n in range(len(wanted)):
-            below = jnp.sum((accs[n][0] + accs[n][1]).astype(f32), axis=1, keepdims=True)
-            passed = jnp.where((below < wanted[n].astype(f32)) & (subs[:, :1] < SUBS - 1), 1, 0)
-            digit = jnp.sum(passed, axis=0, keepdims=True)
-            base[n] = base[n] + (jnp.broadcast_to(digit, (SUBS, LANES)) << shift)
+            below = jnp.broadcast_to(jnp.sum((accs[n][0] + accs[n][1]).astype(f32), axis=1, keepdims=True), (SUBS, LANES))
+            passed = jnp.where((below < wanted[n].astype(f32)) & (subs < SUBS - 1), 1, 0)
+            for turn in (4, 2, 1):
+                passed = passed + pltpu.roll(passed, turn, 0)
+            base[n] = base[n] + (passed << shift)
     return base
 
 
@@ -329,17 +356,16 @@
         k = unpacked(tile)
         code = codes[:, h * LANES : (h + 1) * LANES]
         is_low, is_high = code & 3, (code >> 2) & 3
-        ok = code >= 16
-        ok = ok & ((is_low == 0) | (k >= low + is_low - 1))
-        ok = ok & ((is_high == 0) | (k < high + is_high - 1))
-        keys.append(jnp.where(ok, k, BIG))
+        over = (code < 16) | ((is_high > 0) & (k >= high + is_high - 1))
+        under = (is_low > 0) & (k < low + is_low - 1)
+        keys.append(jnp.where(over, BIG, jnp.where(under, -1, k)))
     return keys
 
 
 def place_kernel(found_ref, keys_out, values_out, size_out, digest_out):
     found = [found_ref[n * SUBS : (n + 1) * SUBS, :] for n in range(6)]
     keys, values, ranks = found[:2], found[2:4], found[4:]
-    valid = jnp.where(keys[0] < BIG, 1, 0) + jnp.where(keys[1] < BIG, 1, 0)
+    valid = sum(jnp.where((k >= 0) & (k < BIG), 1, 0) for k in keys)
     size = jnp.sum(jnp.sum(valid, axis=1, keepdims=True), axis=0, keepdims=True)
     count = 2 * SUBS
     keys, values = placed(
@@ -376,6 +402,8 @@
             dma((2,)),
             dma,
             dma,
+            dma,
+            dma,
             dma((2,)),
             dma((2, AXIS)),
             dma((2, AXIS)),

time: 23 us -> 22.6 us (0.983)
  Pallas kernels: 22.3 us -> 21.8 us
    pallas_call x1, Pallas kernels: 21.3 us -> 20.9 us  [candidates(): pl.pallas_call(gather_kernel, out_shape=jax.ShapeDtypeStruct((6 * SUBS, L...]
where the time goes in v6:
time: 22.6 us; the launch traced here: 22.5 us
  Pallas kernels  21.8 us (96%)
  between operations  0.64 us (3%)
    pallas_call x1, Pallas kernels, candidates(): pl.pallas_call(gather_kernel, out_shape=jax.ShapeDtypeStruct((6 * SUBS, L...  20.9 us
    pallas_call x1, Pallas kernels, placed_bucket(): pl.pallas_call(place_kernel, out_shape=(jax.ShapeDtypeStruct((rows, LANES...  0.96 us

profile of v6, /device:TPU:1, one launch (start us, length us, event | category | flops | bytes accessed | tf_op | source)
XLA Modules:
  0.0 22.5 jit_solution(16136696967987135565)
XLA Ops:
  0.6 20.9 %find_candidates.1.found_ref = s32[48,128]{1,0:T(8,128)S(1)} custom-call(s32[8,128]{1,0:T(8,128)} %bitcast.4, s32[8,128]{1,0:T(8,128)} %bitcast.5), custom_call_target="tpu_custom_call" | custom-call | tf_op jit(solution)/shard_map/find_candidates/pallas_call | solution.py:389
  21.5 1.0 %place_bucket.1 = (s32[15,128]{1,0:T(8,128)}, s32[15,128]{1,0:T(8,128)}, s32[1]{0:T(128)}, s32[1]{0:T(128)}) custom-call(s32[48,128]{1,0:T(8,128)S(1)} %find_candidates.1.found_ref), custom_call_target="tpu_custom_call" | custom-call | tf_op jit(solution)/shard_map/place_bucket/pallas_call | solution.py:419

commit v7 on v6

--- a/solution.py
+++ b/solution.py
@@ -246,8 +246,9 @@
     key_gives = forward(0)
     low, high = search(rows, wanted, ends, SHIFTS[EARLY:])
     high = jnp.where(me == devices - 1, BIG, high)
-    codes = group_plan(wanted, low, high, rows, turns, inside)
+    plan = group_plan(wanted, low, high, rows, turns, inside)
     tiles = collect([zero] * 2, blocks, 0, turns, inside, core)
+    codes = column_codes(plan, inside)
     value_gives = forward(1)
     for give in key_gives:
         give.wait_recv()
@@ -293,45 +294,52 @@
     return base
 
 
+def mm(a, b):
+    return jnp.dot(a, b, preferred_element_type=f32)
+
+
 def group_plan(wanted, low, high, rows_ref, turn_ref, in_ref):
     square = (LANES, LANES)
     samples = rows_ref[...].reshape(square)
-    ends = [jnp.broadcast_to(k[:1, :], square) for k in (low, high)]
     ones = jnp.ones(square, bf16)
     below = jnp.where(iota(square, 1) < iota(square, 0), 1.0, 0.0).astype(bf16)
-
-    def mm(a, b):
-        return jnp.dot(a, b, preferred_element_type=f32)
-
     masks = []
-    for k in ends:
-        masks += [samples < k, samples <= k]
+    for k in (low, high):
+        k = jnp.broadcast_to(k[:1, :], square)
+        masks += [samples < k, samples == k]
     counts = mm(jnp.concatenate([jnp.where(m, 1.0, 0.0).astype(bf16) for m in masks], axis=0), ones)
     counts = [counts[n * LANES : (n + 1) * LANES, :] for n in range(4)]
-    taken, tied = [], []
+    left_hand = jnp.concatenate([below, ones[: 2 * SUBS, :]], axis=0)
+    sums = mm(left_hand, jnp.concatenate(counts, axis=1).astype(bf16))
+    taken, tied, before = [], [], []
     for n in range(2):
-        lt, le = counts[2 * n], counts[2 * n + 1]
-        equal = le - lt
-        before = mm(below, equal.astype(bf16))
-        total = mm(ones, lt.astype(bf16))
-        left = jnp.asarray(wanted[n], f32) - total - before
-        taken.append(lt + jnp.clip(left, 0.0, equal))
+        less, equal = counts[2 * n], counts[2 * n + 1]
+        less_before, equal_before = (sums[:LANES, c * LANES : (c + 1) * LANES] for c in (2 * n, 2 * n + 1))
+        total = jnp.broadcast_to(sums[LANES : LANES + 1, 2 * n * LANES : (2 * n + 1) * LANES], square)
+        ties = jnp.asarray(wanted[n], f32) - total
+        left = ties - equal_before
+        taken.append((less + jnp.clip(left, 0.0, equal)).astype(i32))
         tied.append(jnp.where(left > equal, 1, 0))
-    first = taken[0]
-    number = jnp.minimum(taken[1], LANES - 1.0) - first + 1.0
-    start = mm(below, number.astype(bf16)).astype(i32)
-    number, first, last = number.astype(i32), first.astype(i32), taken[1].astype(i32)
+        before.append(less_before + jnp.minimum(ties, equal_before))
+    first, last = taken
+    start = (before[1] - before[0]).astype(i32) + iota(square, 0)
     lanes = iota(square, 1)
     turn_ref[...] = (lanes - (start - first)) & (LANES - 1)
+    for h in range(2):
+        m = lanes + h * LANES
+        in_ref[h] = jnp.where((m >= start) & (m <= start + last - first), 1, 0)
+    return start, first, last, tied
+
+
+def column_codes(plan, in_ref):
+    start, first, last, tied = plan
+    lanes = iota((LANES, LANES), 1)
     codes = []
     for h in range(2):
         m = lanes + h * LANES
-        inside = (m >= start) & (m < start + number)
-        in_ref[h] = jnp.where(inside, 1, 0)
-        code = jnp.where(inside, 16, 0)
-        code = code + jnp.where(inside & (m == start), 1 + tied[0], 0)
-        code = code + jnp.where(inside & (m == start + last - first), 4 * (1 + tied[1]), 0)
-        codes.append(code.astype(f32).astype(bf16))
+        inside = (in_ref[h] > 0) & (m - start + first < LANES)
+        code = jnp.where(m == start, 17 + tied[0], 16) + jnp.where(m == start + last - first, 4 * (1 + tied[1]), 0)
+        codes.append(jnp.where(inside, code, 0).astype(f32).astype(bf16))
     return mm(jnp.ones((SUBS, LANES), bf16), jnp.concatenate(codes, axis=1)).astype(i32)
 
 

time: 22.6 us -> 22.5 us (level)
  no operation moved by 1% of the time
where the time goes in v7:
time: 22.5 us; the launch traced here: 22.4 us
  Pallas kernels  21.8 us (97%)
  between operations  0.64 us (3%)
    pallas_call x1, Pallas kernels, candidates(): pl.pallas_call(gather_kernel, out_shape=jax.ShapeDtypeStruct((6 * SUBS, L...  20.8 us
    pallas_call x1, Pallas kernels, placed_bucket(): pl.pallas_call(place_kernel, out_shape=(jax.ShapeDtypeStruct((rows, LANES...  0.96 us

profile of v7, /device:TPU:1, one launch (start us, length us, event | category | flops | bytes accessed | tf_op | source)
XLA Modules:
  0.0 22.4 jit_solution(6289082390738568437)
XLA Ops:
  0.6 20.8 %find_candidates.1.found_ref = s32[48,128]{1,0:T(8,128)S(1)} custom-call(s32[8,128]{1,0:T(8,128)} %bitcast.4, s32[8,128]{1,0:T(8,128)} %bitcast.5), custom_call_target="tpu_custom_call" | custom-call | tf_op jit(solution)/shard_map/find_candidates/pallas_call | solution.py:397
  21.4 1.0 %place_bucket.1 = (s32[15,128]{1,0:T(8,128)}, s32[15,128]{1,0:T(8,128)}, s32[1]{0:T(128)}, s32[1]{0:T(128)}) custom-call(s32[48,128]{1,0:T(8,128)S(1)} %find_candidates.1.found_ref), custom_call_target="tpu_custom_call" | custom-call | tf_op jit(solution)/shard_map/place_bucket/pallas_call | solution.py:427
